TPU v7x, 32 devices: a whole 2x2x4 slice. The times are simulated.
32 devices in a mesh: dom: 8 (over y, x, core), rep: 4 (over z).
Axes of the slice: x: 2, y: 2, z: 4, core: 2. Of those that a mesh axis runs over, the one named last changes fastest.
Arguments:
- right_sides: float32 [4, 48, 16, 384], P(None, 'dom', 'rep'), may hold values from -6 to 6
- diag_inverse: bfloat16 [4, 48, 384, 384], P(None, 'dom'), may hold values from -0.3125 to 0.3125
- panel_mats: bfloat16 [3, 512, 384, 384], P(None, ('dom', 'rep')), may hold values from -0.08984375 to 0.08984375
- panel_src: int32 [3, 512], P(None, ('dom', 'rep')), may hold values from 0 to 17, as said below
- panel_dst: int32 [3, 512], P(None, ('dom', 'rep')), may hold values from -1 to 47, as said below
Outputs:
- solution: float32 [4, 48, 16, 384], P(None, 'dom', 'rep')
Inputs may be any that keep to these rules, and one draw needn't show every extreme that they name: `panel_src`: an entry of row l is below (l + 1) * 6, so the source tile lies in a level at most l; most of the entries lie in level l itself. A live entry of a list owned by dom index o names a tile of dom index (o + j) mod 8 with -2 <= j <= 2 or j = 4. Among the 16 entries of one device's list for one row, at most 3 live entries have the same destination dom index (panel_dst // 6), and in every list some dom index has exactly 3; lists of low dom indices tend to hold more live entries than those of high ones.
All inputs are finite; a program needn't handle non-finite values.
Results may differ from a plain program's by a relative error of at most 0.012.
Values may be sent and summed in bfloat16 or wider, within the bound.
A program may use at most 128 MiB of HBM per device.

v0:
```python
import jax
import jax.numpy as jnp
from jax import lax
from jax.sharding import PartitionSpec as P

HALF = 2
SLOTS = 3


def passed_along(value, axis, by):
    size = lax.axis_size(axis)
    return lax.ppermute(value, axis, [(i, (i + by) % size) for i in range(size)])


def panel_updates(solved_store, matrices, source_ids):
    sources = solved_store[source_ids]
    return jnp.einsum("pcx,pxy->pcy", sources, matrices, preferred_element_type=jnp.float32)


def deliver(contribution, destinations, tile_count, col_count):
    highest = lax.Precision.HIGHEST
    dom_size = lax.axis_size("dom")
    rep_size = lax.axis_size("rep")
    panel_count = contribution.shape[0]
    span_width = contribution.shape[2]
    split_cols = contribution.reshape(panel_count, rep_size, col_count, span_width)
    hood = 2 * HALF + 2
    far_offset = dom_size // 2
    owner = lax.axis_index("dom")
    is_live = destinations >= 0
    target = jnp.where(is_live, destinations // tile_count, -1)
    distance = (target - owner) % dom_size
    reach = jnp.where(distance == far_offset, hood - 1, (distance + HALF) % dom_size)
    dest_slot = destinations % tile_count
    positions = jnp.arange(panel_count, dtype=jnp.int32)
    earlier = (
        (target[:, None] == target[None, :])
        & is_live[None, :]
        & (positions[None, :] < positions[:, None])
    )
    ranking = jnp.sum(earlier.astype(jnp.int32), axis=1)
    placing = (
        is_live[:, None, None]
        & (reach[:, None, None] == jnp.arange(hood, dtype=jnp.int32)[None, :, None])
        & (ranking[:, None, None] == jnp.arange(SLOTS, dtype=jnp.int32)[None, None, :])
    )
    slot_vals = jnp.einsum(
        "pjk,prcx->jkrcx", placing.astype(jnp.float32), split_cols, precision=highest
    )
    slot_ids = jnp.sum(jnp.where(placing, dest_slot[:, None, None] + 1, 0), axis=0) - 1
    slot_ids = jnp.broadcast_to(slot_ids[:, :, None], (hood, SLOTS, rep_size)).astype(jnp.float32)
    got_vals, got_ids = (
        lax.all_to_all(
            slot_vals.astype(jnp.bfloat16), "rep", split_axis=2, concat_axis=2, tiled=True
        ).astype(slot_vals.dtype),
        lax.all_to_all(
            slot_ids.astype(jnp.bfloat16), "rep", split_axis=2, concat_axis=2, tiled=True
        ).astype(slot_ids.dtype),
    )
    tile_range = jnp.arange(tile_count, dtype=jnp.float32)
    total = jnp.zeros((tile_count, col_count, span_width), jnp.float32)
    for reach_index in range(hood):
        offset = far_offset if reach_index == hood - 1 else reach_index - HALF
        piece_vals = got_vals[reach_index]
        piece_ids = got_ids[reach_index]
        if offset != 0:
            piece_vals, piece_ids = (
                passed_along(piece_vals.astype(jnp.bfloat16), "dom", offset).astype(
                    piece_vals.dtype
                ),
                passed_along(piece_ids.astype(jnp.bfloat16), "dom", offset).astype(piece_ids.dtype),
            )
        picker = (piece_ids[:, :, None] == tile_range[None, None, :]).astype(jnp.float32)
        total = total + jnp.einsum("kns,kncx->scx", picker, piece_vals, precision=highest)
    return total


def per_device(right_sides, diag_inverse, panel_mats, panel_src, panel_dst):
    level_count, tile_count, col_count, span_width = right_sides.shape
    rep_size = lax.axis_size("rep")
    solved_store = jnp.zeros(
        (level_count * tile_count, col_count * rep_size, span_width), jnp.bfloat16
    )
    results = []
    for level_index in range(level_count):
        residual = right_sides[level_index]
        if level_index > 0:
            contribution = panel_updates(
                solved_store, panel_mats[level_index - 1], panel_src[level_index - 1]
            )
            incoming = deliver(contribution, panel_dst[level_index - 1], tile_count, col_count)
            residual = residual - incoming
        solved = jnp.einsum(
            "scx,sxy->scy",
            residual.astype(jnp.bfloat16),
            diag_inverse[level_index],
            preferred_element_type=jnp.float32,
        )
        results.append(solved)
        if level_index + 1 < level_count:
            gathered = lax.all_gather(solved.astype(jnp.bfloat16), "rep", axis=1, tiled=True)
            solved_store = lax.dynamic_update_slice_in_dim(
                solved_store, gathered, level_index * tile_count, 0
            )
    return jnp.stack(results)


def solution(mesh):
    return jax.shard_map(
        per_device,
        mesh=mesh,
        in_specs=(
            P(None, "dom", "rep", None),
            P(None, "dom", None, None),
            P(None, ("dom", "rep"), None, None),
            P(None, ("dom", "rep")),
            P(None, ("dom", "rep")),
        ),
        out_specs=P(None, "dom", "rep", None),
        check_vma=False,
    )
```

profile of v0, /device:TPU:0, one launch (start us, length us, event | category | flops | bytes accessed | tf_op | source)
XLA Modules:
  0.0 155.9 jit_solution(2920154369858025139)
XLA Ops:
  3.7 6.3 %all-to-all-start = ((bf16[6,3,4]{0,1,2:T(4,128)(2,1)}), bf16[6,3,4]{0,1,2:T(4,128)(2,1)S(1)}, u32[]{:S(2)}, u32[]{:S(2)}) async-start(bf16[6,3,4]{0,1,2:T(4,128)(2,1)} %broadcast_in_dim.43), calls=%async_computation | async-start | bytes 8192 | tf_op jit(solution)/shard_map/all_to_all | solution.py:56
  10.8 1.9 %fusion.150 = (bf16[6,4,384]{2,1,0:T(4,128)(2,1)S(1)}, f32[6,4,384]{2,1,0:T(4,128)S(1)}) fusion(bf16[4,6,384,384]{3,2,1,0:T(8,128)(2,1)} %param.6, f32[4,6,4,384]{3,2,1,0:T(4,128)} %param.5), kind=kOutput, calls=%fused_computation.266 | convolution fusion | flops 7087104 | bytes 1843200 | tf_op jit(solution)/shard_map/scx,sxy->scy/dot_general | solution.py:93
  12.7 13.8 %all_gather.9 = bf16[6,16,384]{2,0,1:T(8,128)(2,1)S(1)} all-gather(bf16[6,4,384]{2,0,1:T(8,128)(2,1)S(1)} %copy.230), channel_id=1, replica_groups=mesh['dom'=8,'rep'=4] {'rep'}, dimensions={1}, use_global_device_ids=true | all-gather | bytes 92160 | tf_op jit(solution)/shard_map/all_gather | solution.py:101
  28.0 3.1 %fusion.4 = f32[16,16,384]{2,1,0:T(8,128)S(1)} fusion(bf16[16,16,384]{2,1,0:T(8,128)(2,1)S(1)} %gather_fusion, bf16[3,16,384,384]{3,2,1,0:T(8,128)(2,1)} %param.7), kind=kOutput, calls=%fused_computation.7 | convolution fusion | flops 75497472 | bytes 5308416 | tf_op jit(solution)/shard_map/pcx,pxy->pcy/dot_general | solution.py:17
  32.8 4.6 %all-to-all-start.1 = ((bf16[6,3,4,4,384]{4,3,1,0,2:T(4,128)(2,1)}), bf16[6,3,4,4,384]{4,3,1,0,2:T(4,128)(2,1)S(1)}, u32[]{:S(2)}, u32[]{:S(2)}) async-start(bf16[6,3,4,4,384]{4,3,1,0,2:T(4,128)(2,1)} %copy.233), calls=%async_computation.1 | async-start | bytes 442368 | tf_op jit(solution)/shard_map/all_to_all | solution.py:53
  39.3 2.6 %collective-permute-start.2 = (bf16[3,4]{1,0:T(4,128)(2,1)S(1)}, bf16[3,4]{1,0:T(4,128)(2,1)S(1)}, u32[]{:S(2)}, u32[]{:S(2)}) collective-permute-start(bf16[3,4]{1,0:T(4,128)(2,1)S(1)} %bitcast.404), channel_id=1, source_target_pairs={{0,28},{4,0},{8,4},{12,8},{16,12},{20,16},{24,20},{28,24},{1,29},{... | collective-permute-start | bytes 80 | tf_op jit(solution)/shard_map/ppermute | solution.py:12
  48.0 5.1 %all-to-all-start.2 = ((bf16[6,3,4]{0,1,2:T(4,128)(2,1)}), bf16[6,3,4]{0,1,2:T(4,128)(2,1)S(1)}, u32[]{:S(2)}, u32[]{:S(2)}) async-start(bf16[6,3,4]{0,1,2:T(4,128)(2,1)} %broadcast_in_dim.45), calls=%async_computation.2 | async-start | bytes 8192 | tf_op jit(solution)/shard_map/all_to_all | solution.py:56
  53.8 2.7 %collective-permute-start.3 = (bf16[3,4,4,384]{3,1,0,2:T(4,128)(2,1)S(1)}, bf16[3,4,4,384]{3,1,0,2:T(4,128)(2,1)S(1)}, u32[]{:S(2)}, u32[]{:S(2)}) collective-permute-start(bf16[3,4,4,384]{3,1,0,2:T(4,128)(2,1)S(1)} %copy.238), channel_id=1, source_target_pairs={{0,28},{4,0},{8,4},{12,8},{16,12},{20,16},{24,20},{28,24},{1,29},{... | collective-permute-start | bytes 110600 | tf_op jit(solution)/shard_map/ppermute | solution.py:12
  62.4 1.8 %fusion.151 = (bf16[6,4,384]{2,1,0:T(4,128)(2,1)S(1)}, f32[6,4,384]{2,1,0:T(4,128)S(1)}) fusion(bf16[4,6,384,384]{3,2,1,0:T(8,128)(2,1)} %param.6, bf16[6,4,384]{2,0,1:T(8,128)(2,1)S(1)} %fusion.44), kind=kOutput, calls=%fused_computation.267 | convolution fusion | flops 7087104 | bytes 1843200 | tf_op jit(solution)/shard_map/scx,sxy->scy/dot_general | solution.py:93
  64.3 13.8 %all_gather.10 = bf16[6,16,384]{2,0,1:T(8,128)(2,1)S(1)} all-gather(bf16[6,4,384]{2,0,1:T(8,128)(2,1)S(1)} %copy.254), channel_id=1, replica_groups=mesh['dom'=8,'rep'=4] {'rep'}, dimensions={1}, use_global_device_ids=true | all-gather | bytes 92160 | tf_op jit(solution)/shard_map/all_gather | solution.py:101
  78.7 3.1 %fusion.2 = f32[16,16,384]{2,1,0:T(8,128)S(1)} fusion(bf16[16,16,384]{2,1,0:T(8,128)(2,1)S(1)} %gather_fusion.1, bf16[3,16,384,384]{3,2,1,0:T(8,128)(2,1)} %param.7), kind=kOutput, calls=%fused_computation.5 | convolution fusion | flops 75497472 | bytes 5308416 | tf_op jit(solution)/shard_map/pcx,pxy->pcy/dot_general | solution.py:17
  83.2 4.6 %all-to-all-start.3 = ((bf16[6,3,4,4,384]{4,3,1,0,2:T(4,128)(2,1)}), bf16[6,3,4,4,384]{4,3,1,0,2:T(4,128)(2,1)S(1)}, u32[]{:S(2)}, u32[]{:S(2)}) async-start(bf16[6,3,4,4,384]{4,3,1,0,2:T(4,128)(2,1)} %copy.257), calls=%async_computation.3 | async-start | bytes 442368 | tf_op jit(solution)/shard_map/all_to_all | solution.py:53
  95.0 5.1 %all-to-all-start.4 = ((bf16[6,3,4]{0,1,2:T(4,128)(2,1)}), bf16[6,3,4]{0,1,2:T(4,128)(2,1)S(1)}, u32[]{:S(2)}, u32[]{:S(2)}) async-start(bf16[6,3,4]{0,1,2:T(4,128)(2,1)} %broadcast_in_dim.47), calls=%async_computation.4 | async-start | bytes 8192 | tf_op jit(solution)/shard_map/all_to_all | solution.py:56
  100.2 1.8 %collective-permute-start.13 = (bf16[3,4,4,384]{3,1,0,2:T(4,128)(2,1)S(1)}, bf16[3,4,4,384]{3,1,0,2:T(4,128)(2,1)S(1)}, u32[]{:S(2)}, u32[]{:S(2)}) collective-permute-start(bf16[3,4,4,384]{3,1,0,2:T(4,128)(2,1)S(1)} %copy.262), channel_id=1, source_target_pairs={{0,28},{4,0},{8,4},{12,8},{16,12},{20,16},{24,20},{28,24},{1,29},{... | collective-permute-start | bytes 110600 | tf_op jit(solution)/shard_map/ppermute | solution.py:12
  103.8 3.0 %collective-permute-start.11 = (bf16[3,4,4,384]{3,1,0,2:T(4,128)(2,1)S(1)}, bf16[3,4,4,384]{3,1,0,2:T(4,128)(2,1)S(1)}, u32[]{:S(2)}, u32[]{:S(2)}) collective-permute-start(bf16[3,4,4,384]{3,1,0,2:T(4,128)(2,1)S(1)} %copy.259), channel_id=1, source_target_pairs={{0,24},{4,28},{8,0},{12,4},{16,8},{20,12},{24,16},{28,20},{1,25},{... | collective-permute-start | bytes 110600 | tf_op jit(solution)/shard_map/ppermute | solution.py:12
  108.7 1.8 %fusion.152 = (bf16[6,4,384]{2,1,0:T(4,128)(2,1)S(1)}, f32[6,4,384]{2,1,0:T(4,128)S(1)}) fusion(bf16[4,6,384,384]{3,2,1,0:T(8,128)(2,1)} %param.6, bf16[6,4,384]{2,0,1:T(8,128)(2,1)S(1)} %fusion.43), kind=kOutput, calls=%fused_computation.268 | convolution fusion | flops 7087104 | bytes 1843200 | tf_op jit(solution)/shard_map/scx,sxy->scy/dot_general | solution.py:93
  110.5 13.5 %all_gather.11 = bf16[6,16,384]{2,0,1:T(8,128)(2,1)S(1)} all-gather(bf16[6,4,384]{2,0,1:T(8,128)(2,1)S(1)} %copy.278), channel_id=1, replica_groups=mesh['dom'=8,'rep'=4] {'rep'}, dimensions={1}, use_global_device_ids=true | all-gather | bytes 92160 | tf_op jit(solution)/shard_map/all_gather | solution.py:101
  124.7 3.1 %fusion = f32[16,16,384]{2,1,0:T(8,128)S(1)} fusion(bf16[16,16,384]{2,1,0:T(8,128)(2,1)S(1)} %gather_fusion.2, bf16[3,16,384,384]{3,2,1,0:T(8,128)(2,1)} %param.7), kind=kOutput, calls=%fused_computation.3 | convolution fusion | flops 75497472 | bytes 5308416 | tf_op jit(solution)/shard_map/pcx,pxy->pcy/dot_general | solution.py:17
  129.1 4.6 %all-to-all-start.5 = ((bf16[6,3,4,4,384]{4,3,1,0,2:T(4,128)(2,1)}), bf16[6,3,4,4,384]{4,3,1,0,2:T(4,128)(2,1)S(1)}, u32[]{:S(2)}, u32[]{:S(2)}) async-start(bf16[6,3,4,4,384]{4,3,1,0,2:T(4,128)(2,1)} %copy.281), calls=%async_computation.5 | async-start | bytes 442368 | tf_op jit(solution)/shard_map/all_to_all | solution.py:53
  133.9 2.5 %collective-permute-start.26 = (bf16[3,4]{1,0:T(4,128)(2,1)S(1)}, bf16[3,4]{1,0:T(4,128)(2,1)S(1)}, u32[]{:S(2)}, u32[]{:S(2)}) collective-permute-start(bf16[3,4]{1,0:T(4,128)(2,1)S(1)} %bitcast.408), channel_id=1, source_target_pairs={{0,8},{4,12},{8,16},{12,20},{16,24},{20,28},{24,0},{28,4},{1,9},{5... | collective-permute-start | bytes 80 | tf_op jit(solution)/shard_map/ppermute | solution.py:12
  136.7 2.6 %collective-permute-start.22 = (bf16[3,4]{1,0:T(4,128)(2,1)S(1)}, bf16[3,4]{1,0:T(4,128)(2,1)S(1)}, u32[]{:S(2)}, u32[]{:S(2)}) collective-permute-start(bf16[3,4]{1,0:T(4,128)(2,1)S(1)} %bitcast.410), channel_id=1, source_target_pairs={{0,28},{4,0},{8,4},{12,8},{16,12},{20,16},{24,20},{28,24},{1,29},{... | collective-permute-start | bytes 80 | tf_op jit(solution)/shard_map/ppermute | solution.py:12
  141.0 2.0 %collective-permute-done.28 = bf16[3,4]{1,0:T(4,128)(2,1)S(1)} collective-permute-done((bf16[3,4]{1,0:T(4,128)(2,1)S(1)}, bf16[3,4]{1,0:T(4,128)(2,1)S(1)}, u32[]{:S(2)}, u32[]{:S(2)}) %collective-permute-start.28) | collective-permute-done | bytes 56 | tf_op jit(solution)/shard_map/ppermute | solution.py:12
  145.0 2.7 %collective-permute-start.23 = (bf16[3,4,4,384]{3,1,0,2:T(4,128)(2,1)S(1)}, bf16[3,4,4,384]{3,1,0,2:T(4,128)(2,1)S(1)}, u32[]{:S(2)}, u32[]{:S(2)}) collective-permute-start(bf16[3,4,4,384]{3,1,0,2:T(4,128)(2,1)S(1)} %copy.286), channel_id=1, source_target_pairs={{0,28},{4,0},{8,4},{12,8},{16,12},{20,16},{24,20},{28,24},{1,29},{... | collective-permute-start | bytes 110600 | tf_op jit(solution)/shard_map/ppermute | solution.py:12
  153.3 1.8 %fusion.39 = f32[1,6,4,384]{3,2,1,0:T(4,128)S(1)} fusion(bf16[4,6,384,384]{3,2,1,0:T(8,128)(2,1)} %param.6, bf16[6,4,384]{2,0,1:T(8,128)(2,1)S(1)} %fusion.42), kind=kOutput, calls=%fused_computation.63 | convolution fusion | flops 7077888 | bytes 1824768 | tf_op jit(solution)/shard_map/scx,sxy->scy/dot_general | solution.py:93
  (178 shorter events, 47.4 us)
Async XLA Ops:
  3.7 29.1 %all-to-all-start = ((bf16[6,3,4]{0,1,2:T(4,128)(2,1)}), bf16[6,3,4]{0,1,2:T(4,128)(2,1)S(1)}, u32[]{:S(2)}, u32[]{:S(2)}) async-start(bf16[6,3,4]{0,1,2:T(4,128)(2,1)} %broadcast_in_dim.43), calls=%async_computation | async-start | bytes 8192 | tf_op jit(solution)/shard_map/all_to_all | solution.py:56
  32.8 14.6 %all-to-all-start.1 = ((bf16[6,3,4,4,384]{4,3,1,0,2:T(4,128)(2,1)}), bf16[6,3,4,4,384]{4,3,1,0,2:T(4,128)(2,1)S(1)}, u32[]{:S(2)}, u32[]{:S(2)}) async-start(bf16[6,3,4,4,384]{4,3,1,0,2:T(4,128)(2,1)} %copy.233), calls=%async_computation.1 | async-start | bytes 442368 | tf_op jit(solution)/shard_map/all_to_all | solution.py:53
  37.6 6.8 %collective-permute-start.6 = (bf16[3,4]{1,0:T(4,128)(2,1)S(1)}, bf16[3,4]{1,0:T(4,128)(2,1)S(1)}, u32[]{:S(2)}, u32[]{:S(2)}) collective-permute-start(bf16[3,4]{1,0:T(4,128)(2,1)S(1)} %bitcast.402), channel_id=1, source_target_pairs={{0,8},{4,12},{8,16},{12,20},{16,24},{20,28},{24,0},{28,4},{1,9},{5... | collective-permute-start | bytes 80 | tf_op jit(solution)/shard_map/ppermute | solution.py:12
  39.2 5.2 %collective-permute-start.4 = (bf16[3,4]{1,0:T(4,128)(2,1)S(1)}, bf16[3,4]{1,0:T(4,128)(2,1)S(1)}, u32[]{:S(2)}, u32[]{:S(2)}) collective-permute-start(bf16[3,4]{1,0:T(4,128)(2,1)S(1)} %bitcast.403), channel_id=1, source_target_pairs={{0,4},{4,8},{8,12},{12,16},{16,20},{20,24},{24,28},{28,0},{1,5},{5... | collective-permute-start | bytes 80 | tf_op jit(solution)/shard_map/ppermute | solution.py:12
  39.3 5.1 %collective-permute-start.2 = (bf16[3,4]{1,0:T(4,128)(2,1)S(1)}, bf16[3,4]{1,0:T(4,128)(2,1)S(1)}, u32[]{:S(2)}, u32[]{:S(2)}) collective-permute-start(bf16[3,4]{1,0:T(4,128)(2,1)S(1)} %bitcast.404), channel_id=1, source_target_pairs={{0,28},{4,0},{8,4},{12,8},{16,12},{20,16},{24,20},{28,24},{1,29},{... | collective-permute-start | bytes 80 | tf_op jit(solution)/shard_map/ppermute | solution.py:12
  48.0 35.2 %all-to-all-start.2 = ((bf16[6,3,4]{0,1,2:T(4,128)(2,1)}), bf16[6,3,4]{0,1,2:T(4,128)(2,1)S(1)}, u32[]{:S(2)}, u32[]{:S(2)}) async-start(bf16[6,3,4]{0,1,2:T(4,128)(2,1)} %broadcast_in_dim.45), calls=%async_computation.2 | async-start | bytes 8192 | tf_op jit(solution)/shard_map/all_to_all | solution.py:56
  53.2 5.8 %collective-permute-start.7 = (bf16[3,4,4,384]{3,1,0,2:T(4,128)(2,1)S(1)}, bf16[3,4,4,384]{3,1,0,2:T(4,128)(2,1)S(1)}, u32[]{:S(2)}, u32[]{:S(2)}) collective-permute-start(bf16[3,4,4,384]{3,1,0,2:T(4,128)(2,1)S(1)} %copy.247), channel_id=1, source_target_pairs={{0,8},{4,12},{8,16},{12,20},{16,24},{20,28},{24,0},{28,4},{1,9},{5... | collective-permute-start | bytes 110600 | tf_op jit(solution)/shard_map/ppermute | solution.py:12
  53.8 5.5 %collective-permute-start.5 = (bf16[3,4,4,384]{3,1,0,2:T(4,128)(2,1)S(1)}, bf16[3,4,4,384]{3,1,0,2:T(4,128)(2,1)S(1)}, u32[]{:S(2)}, u32[]{:S(2)}) collective-permute-start(bf16[3,4,4,384]{3,1,0,2:T(4,128)(2,1)S(1)} %copy.244), channel_id=1, source_target_pairs={{0,4},{4,8},{8,12},{12,16},{16,20},{20,24},{24,28},{28,0},{1,5},{5... | collective-permute-start | bytes 110600 | tf_op jit(solution)/shard_map/ppermute | solution.py:12
  53.8 5.7 %collective-permute-start.3 = (bf16[3,4,4,384]{3,1,0,2:T(4,128)(2,1)S(1)}, bf16[3,4,4,384]{3,1,0,2:T(4,128)(2,1)S(1)}, u32[]{:S(2)}, u32[]{:S(2)}) collective-permute-start(bf16[3,4,4,384]{3,1,0,2:T(4,128)(2,1)S(1)} %copy.238), channel_id=1, source_target_pairs={{0,28},{4,0},{8,4},{12,8},{16,12},{20,16},{24,20},{28,24},{1,29},{... | collective-permute-start | bytes 110600 | tf_op jit(solution)/shard_map/ppermute | solution.py:12
  83.2 11.2 %all-to-all-start.3 = ((bf16[6,3,4,4,384]{4,3,1,0,2:T(4,128)(2,1)}), bf16[6,3,4,4,384]{4,3,1,0,2:T(4,128)(2,1)S(1)}, u32[]{:S(2)}, u32[]{:S(2)}) async-start(bf16[6,3,4,4,384]{4,3,1,0,2:T(4,128)(2,1)} %copy.257), calls=%async_computation.3 | async-start | bytes 442368 | tf_op jit(solution)/shard_map/all_to_all | solution.py:53
  88.1 4.5 %collective-permute-start.16 = (bf16[3,4]{1,0:T(4,128)(2,1)S(1)}, bf16[3,4]{1,0:T(4,128)(2,1)S(1)}, u32[]{:S(2)}, u32[]{:S(2)}) collective-permute-start(bf16[3,4]{1,0:T(4,128)(2,1)S(1)} %bitcast.406), channel_id=1, source_target_pairs={{0,8},{4,12},{8,16},{12,20},{16,24},{20,28},{24,0},{28,4},{1,9},{5... | collective-permute-start | bytes 80 | tf_op jit(solution)/shard_map/ppermute | solution.py:12
  95.0 34.1 %all-to-all-start.4 = ((bf16[6,3,4]{0,1,2:T(4,128)(2,1)}), bf16[6,3,4]{0,1,2:T(4,128)(2,1)S(1)}, u32[]{:S(2)}, u32[]{:S(2)}) async-start(bf16[6,3,4]{0,1,2:T(4,128)(2,1)} %broadcast_in_dim.47), calls=%async_computation.4 | async-start | bytes 8192 | tf_op jit(solution)/shard_map/all_to_all | solution.py:56
  100.2 6.8 %collective-permute-start.13 = (bf16[3,4,4,384]{3,1,0,2:T(4,128)(2,1)S(1)}, bf16[3,4,4,384]{3,1,0,2:T(4,128)(2,1)S(1)}, u32[]{:S(2)}, u32[]{:S(2)}) collective-permute-start(bf16[3,4,4,384]{3,1,0,2:T(4,128)(2,1)S(1)} %copy.262), channel_id=1, source_target_pairs={{0,28},{4,0},{8,4},{12,8},{16,12},{20,16},{24,20},{28,24},{1,29},{... | collective-permute-start | bytes 110600 | tf_op jit(solution)/shard_map/ppermute | solution.py:12
  102.0 5.3 %collective-permute-start.17 = (bf16[3,4,4,384]{3,1,0,2:T(4,128)(2,1)S(1)}, bf16[3,4,4,384]{3,1,0,2:T(4,128)(2,1)S(1)}, u32[]{:S(2)}, u32[]{:S(2)}) collective-permute-start(bf16[3,4,4,384]{3,1,0,2:T(4,128)(2,1)S(1)} %copy.271), channel_id=1, source_target_pairs={{0,8},{4,12},{8,16},{12,20},{16,24},{20,28},{24,0},{28,4},{1,9},{5... | collective-permute-start | bytes 110600 | tf_op jit(solution)/shard_map/ppermute | solution.py:12
  102.7 4.8 %collective-permute-start.15 = (bf16[3,4,4,384]{3,1,0,2:T(4,128)(2,1)S(1)}, bf16[3,4,4,384]{3,1,0,2:T(4,128)(2,1)S(1)}, u32[]{:S(2)}, u32[]{:S(2)}) collective-permute-start(bf16[3,4,4,384]{3,1,0,2:T(4,128)(2,1)S(1)} %copy.268), channel_id=1, source_target_pairs={{0,4},{4,8},{8,12},{12,16},{16,20},{20,24},{24,28},{28,0},{1,5},{5... | collective-permute-start | bytes 110600 | tf_op jit(solution)/shard_map/ppermute | solution.py:12
  103.0 4.8 %collective-permute-start.19 = (bf16[3,4,4,384]{3,1,0,2:T(4,128)(2,1)S(1)}, bf16[3,4,4,384]{3,1,0,2:T(4,128)(2,1)S(1)}, u32[]{:S(2)}, u32[]{:S(2)}) collective-permute-start(bf16[3,4,4,384]{3,1,0,2:T(4,128)(2,1)S(1)} %copy.274), channel_id=1, source_target_pairs={{0,16},{4,20},{8,24},{12,28},{16,0},{20,4},{24,8},{28,12},{1,17},{... | collective-permute-start | bytes 110600 | tf_op jit(solution)/shard_map/ppermute | solution.py:12
  103.8 4.6 %collective-permute-start.11 = (bf16[3,4,4,384]{3,1,0,2:T(4,128)(2,1)S(1)}, bf16[3,4,4,384]{3,1,0,2:T(4,128)(2,1)S(1)}, u32[]{:S(2)}, u32[]{:S(2)}) collective-permute-start(bf16[3,4,4,384]{3,1,0,2:T(4,128)(2,1)S(1)} %copy.259), channel_id=1, source_target_pairs={{0,24},{4,28},{8,0},{12,4},{16,8},{20,12},{24,16},{28,20},{1,25},{... | collective-permute-start | bytes 110600 | tf_op jit(solution)/shard_map/ppermute | solution.py:12
  129.1 15.4 %all-to-all-start.5 = ((bf16[6,3,4,4,384]{4,3,1,0,2:T(4,128)(2,1)}), bf16[6,3,4,4,384]{4,3,1,0,2:T(4,128)(2,1)S(1)}, u32[]{:S(2)}, u32[]{:S(2)}) async-start(bf16[6,3,4,4,384]{4,3,1,0,2:T(4,128)(2,1)} %copy.281), calls=%async_computation.5 | async-start | bytes 442368 | tf_op jit(solution)/shard_map/all_to_all | solution.py:53
  133.9 7.0 %collective-permute-start.26 = (bf16[3,4]{1,0:T(4,128)(2,1)S(1)}, bf16[3,4]{1,0:T(4,128)(2,1)S(1)}, u32[]{:S(2)}, u32[]{:S(2)}) collective-permute-start(bf16[3,4]{1,0:T(4,128)(2,1)S(1)} %bitcast.408), channel_id=1, source_target_pairs={{0,8},{4,12},{8,16},{12,20},{16,24},{20,28},{24,0},{28,4},{1,9},{5... | collective-permute-start | bytes 80 | tf_op jit(solution)/shard_map/ppermute | solution.py:12
  136.5 4.4 %collective-permute-start.24 = (bf16[3,4]{1,0:T(4,128)(2,1)S(1)}, bf16[3,4]{1,0:T(4,128)(2,1)S(1)}, u32[]{:S(2)}, u32[]{:S(2)}) collective-permute-start(bf16[3,4]{1,0:T(4,128)(2,1)S(1)} %bitcast.409), channel_id=1, source_target_pairs={{0,4},{4,8},{8,12},{12,16},{16,20},{20,24},{24,28},{28,0},{1,5},{5... | collective-permute-start | bytes 80 | tf_op jit(solution)/shard_map/ppermute | solution.py:12
  136.7 4.3 %collective-permute-start.22 = (bf16[3,4]{1,0:T(4,128)(2,1)S(1)}, bf16[3,4]{1,0:T(4,128)(2,1)S(1)}, u32[]{:S(2)}, u32[]{:S(2)}) collective-permute-start(bf16[3,4]{1,0:T(4,128)(2,1)S(1)} %bitcast.410), channel_id=1, source_target_pairs={{0,28},{4,0},{8,4},{12,8},{16,12},{20,16},{24,20},{28,24},{1,29},{... | collective-permute-start | bytes 80 | tf_op jit(solution)/shard_map/ppermute | solution.py:12
  144.6 6.0 %collective-permute-start.27 = (bf16[3,4,4,384]{3,1,0,2:T(4,128)(2,1)S(1)}, bf16[3,4,4,384]{3,1,0,2:T(4,128)(2,1)S(1)}, u32[]{:S(2)}, u32[]{:S(2)}) collective-permute-start(bf16[3,4,4,384]{3,1,0,2:T(4,128)(2,1)S(1)} %copy.295), channel_id=1, source_target_pairs={{0,8},{4,12},{8,16},{12,20},{16,24},{20,28},{24,0},{28,4},{1,9},{5... | collective-permute-start | bytes 110600 | tf_op jit(solution)/shard_map/ppermute | solution.py:12
  144.9 6.0 %collective-permute-start.25 = (bf16[3,4,4,384]{3,1,0,2:T(4,128)(2,1)S(1)}, bf16[3,4,4,384]{3,1,0,2:T(4,128)(2,1)S(1)}, u32[]{:S(2)}, u32[]{:S(2)}) collective-permute-start(bf16[3,4,4,384]{3,1,0,2:T(4,128)(2,1)S(1)} %copy.292), channel_id=1, source_target_pairs={{0,4},{4,8},{8,12},{12,16},{16,20},{20,24},{24,28},{28,0},{1,5},{5... | collective-permute-start | bytes 110600 | tf_op jit(solution)/shard_map/ppermute | solution.py:12
  145.0 6.2 %collective-permute-start.23 = (bf16[3,4,4,384]{3,1,0,2:T(4,128)(2,1)S(1)}, bf16[3,4,4,384]{3,1,0,2:T(4,128)(2,1)S(1)}, u32[]{:S(2)}, u32[]{:S(2)}) collective-permute-start(bf16[3,4,4,384]{3,1,0,2:T(4,128)(2,1)S(1)} %copy.286), channel_id=1, source_target_pairs={{0,28},{4,0},{8,4},{12,8},{16,12},{20,16},{24,20},{28,24},{1,29},{... | collective-permute-start | bytes 110600 | tf_op jit(solution)/shard_map/ppermute | solution.py:12
  (12 other events, 45.7 us)
where the time goes:
time: 157 us; the launch traced here: 156 us
  starting transfers between devices  64.1 us (41%)
  blocking collectives  41.1 us (26%)
  matrix products  22.9 us (15%)
  waiting for transfers between devices  12.3 us (8%)
  local copies, waits for them, and re-layouts  9.84 us (6%)
  other arithmetic  5.2 us (3%)
    all_gather x3, blocking collectives, per_device(): lax.all_gather(solved.astype(jnp.bfloat16), 'rep', axis=1, tiled=True)  41.1 us
    ppermute x30, starting transfers between devices, passed_along(): lax.ppermute(value, axis, [(i, (i + by) % size) for i in range(size)])  33.9 us
    all_to_all x3, starting transfers between devices, deliver(): lax.all_to_all(slot_ids.astype(jnp.bfloat16), 'rep', split_axis=2, concat...  16.5 us
    all_to_all x3, starting transfers between devices, deliver(): lax.all_to_all(slot_vals.astype(jnp.bfloat16), 'rep', split_axis=2, conca...  13.7 us
    ppermute x30, waiting for transfers between devices, passed_along(): lax.ppermute(value, axis, [(i, (i + by) % size) for i in range(size)])  12.3 us
    dot_general x3, matrix products, panel_updates(): jnp.einsum('pcx,pxy->pcy', sources, matrices, preferred_element_type=jnp....  9.38 us
    dot_general x4, matrix products, per_device(): jnp.einsum('scx,sxy->scy', residual.astype(jnp.bfloat16), diag_inverse[le...  7.38 us
    dot_general x18, matrix products, deliver(): jnp.einsum('kns,kncx->scx', picker, piece_vals, precision=highest)  4.87 us
  transfers between devices with their start and end apart: 36, of which 13 were waited for; matrix products, arithmetic and copies ran while one was open for 19% of the time, Pallas kernels for 0%

commit v1 on v0

v1 whole, which is shorter than its diff:
```python
import functools

import jax
import jax.numpy as jnp
import numpy as np
from jax import lax
from jax.experimental import pallas as pl
from jax.experimental.pallas import tpu as pltpu
from jax.sharding import PartitionSpec as P

HALF = 2
SLOTS = 3
HOOD = 2 * HALF + 2
MESH = pl.DeviceIdType.MESH
F32 = jnp.float32
BF16 = jnp.bfloat16


def round_up(value, unit):
    return -(-value // unit) * unit


def iota(shape, dim):
    return lax.broadcasted_iota(jnp.int32, shape, dim).astype(F32)


def lane_tables(rep_size, panel_count, col_count, slot_rows):
    rhs = rep_size * col_count
    width = max(panel_count * rhs, HOOD * rep_size * slot_rows, 128)
    lane = np.arange(width)
    return np.stack(
        [
            lane // rhs,
            (lane % rhs) // col_count * slot_rows + lane % col_count,
            lane // slot_rows,
            (lane % slot_rows) // col_count,
            lane % col_count,
            lane % slot_rows,
            0 * lane,
            0 * lane,
        ]
    ).astype(np.float32)


def regroup_table(rep_size, tile_count, col_count, group_rows):
    table = np.zeros((tile_count * rep_size * col_count, rep_size * group_rows), np.float32)
    for r in range(rep_size):
        for t in range(tile_count):
            for c in range(col_count):
                table[(t * rep_size + r) * col_count + c, r * group_rows + t * col_count + c] = 1
    return table


def kernel(
    dims,
    src_ref, dst_ref, rs_ref, lanes_ref, regroup_ref, diag_hbm, panel_hbm,
    out_ref,
    diag, panel, store, contrib, pack, unpack,
    solved_send, solved_recv, val_send, val_recv, id_send, id_recv,
    diag_sem, panel_sem, solved_ssem, solved_rsem, val_ssem, val_rsem, id_ssem, id_rsem,
):
    levels, tiles, cols, width, panels, dom_size, rep_size, slot_rows, group_rows, chunk = dims
    far = dom_size // 2
    rhs = rep_size * cols
    tile_rows = tiles * cols
    me_d = lax.axis_index("dom")
    me_r = lax.axis_index("rep")
    offsets = [o - HALF for o in range(HOOD - 1)] + [far]
    senders = HOOD * rep_size

    def peer_dom(offset):
        return lax.rem(me_d + (offset + dom_size), dom_size)

    def peer_rep(step):
        return lax.rem(me_r + step, rep_size)

    peers = [
        (j, step)
        for j in (HOOD - 1, 0, HOOD - 2, 1, HOOD - 3, HALF)
        for step in range(rep_size - 1, -1, -1)
        if (offsets[j], step) != (0, 0)
    ]

    def load_diag(level):
        return pltpu.make_async_copy(diag_hbm.at[level], diag.at[level], diag_sem.at[level])

    def load_panel(level, part):
        span = pl.ds(part * chunk, chunk)
        return pltpu.make_async_copy(
            panel_hbm.at[level, span], panel.at[level, span], panel_sem.at[level, part]
        )

    def send_id(j, step):
        return pltpu.make_async_remote_copy(
            src_ref=id_send.at[j],
            dst_ref=id_recv.at[j * rep_size + me_r],
            send_sem=id_ssem.at[j * rep_size + step],
            recv_sem=id_rsem.at[j * rep_size + me_r],
            device_id=(peer_dom(offsets[j]), peer_rep(step)),
            device_id_type=MESH,
        )

    def await_id(j, step):
        slot = j * rep_size + peer_rep(step)
        pltpu.make_async_remote_copy(
            src_ref=id_send.at[j],
            dst_ref=id_recv.at[slot],
            send_sem=id_ssem.at[j * rep_size + step],
            recv_sem=id_rsem.at[slot],
            device_id=(peer_dom(-offsets[j]), peer_rep(step)),
            device_id_type=MESH,
        ).wait_recv()


    def send_val(level, j, step):
        return pltpu.make_async_remote_copy(
            src_ref=val_send.at[level, j * rep_size + peer_rep(step)],
            dst_ref=val_recv.at[level, j * rep_size + me_r],
            send_sem=val_ssem.at[level, j * rep_size + step],
            recv_sem=val_rsem.at[level, j * rep_size + me_r],
            device_id=(peer_dom(offsets[j]), peer_rep(step)),
            device_id_type=MESH,
        )

    def await_val(level, j, step):
        slot = j * rep_size + peer_rep(step)
        pltpu.make_async_remote_copy(
            src_ref=val_send.at[level, slot],
            dst_ref=val_recv.at[level, slot],
            send_sem=val_ssem.at[level, j * rep_size + step],
            recv_sem=val_rsem.at[level, slot],
            device_id=(peer_dom(-offsets[j]), peer_rep(step)),
            device_id_type=MESH,
        ).wait_recv()

    tile_span = pl.ds(0, tile_rows)

    def send_solved(level, step):
        return pltpu.make_async_remote_copy(
            src_ref=solved_send.at[level, tile_span],
            dst_ref=solved_recv.at[level, me_r, tile_span],
            send_sem=solved_ssem.at[level, step],
            recv_sem=solved_rsem.at[level, me_r],
            device_id=(me_d, peer_rep(step)),
            device_id_type=MESH,
        )

    def await_solved(level, step):
        slot = peer_rep(step)
        pltpu.make_async_remote_copy(
            src_ref=solved_send.at[level, tile_span],
            dst_ref=solved_recv.at[level, slot, tile_span],
            send_sem=solved_ssem.at[level, step],
            recv_sem=solved_rsem.at[level, slot],
            device_id=(me_d, slot),
            device_id_type=MESH,
        ).wait_recv()

    load_diag(0).start()

    solved_recv[...] = jnp.zeros_like(solved_recv)

    barrier = pltpu.get_barrier_semaphore()
    for j, step in peers:
        pl.semaphore_signal(
            barrier,
            inc=1,
            device_id=(peer_dom(offsets[j]), peer_rep(step)),
            device_id_type=MESH,
        )

    def route():
        owner = me_d.astype(F32)
        lane_panel = lanes_ref[0:1, : panels * rhs]
        lane_row = lanes_ref[1:2, : panels * rhs]
        id_level = lanes_ref[2:3, :128]
        id_slot = lanes_ref[3:4, :128]
        id_col = lanes_ref[4:5, :128]
        row16 = iota((panels, panels), 0)
        col16 = iota((panels, panels), 1)
        wanted = [jnp.zeros((1, 128), F32) for _ in range(HOOD)]
        for l in range(levels - 1):
            drow = dst_ref[l : l + 1, :].astype(F32)
            dcol = jnp.sum(jnp.where(row16 == col16, drow, 0.0), axis=1, keepdims=True)
            trow = jnp.where(drow >= 0, jnp.floor((drow + 0.5) * (1.0 / tiles)), -1.0)
            tcol = jnp.where(dcol >= 0, jnp.floor((dcol + 0.5) * (1.0 / tiles)), -1.0)
            earlier = (tcol == trow) & (drow >= 0) & (col16 < row16)
            rank = jnp.sum(jnp.where(earlier, 1.0, 0.0), axis=1, keepdims=True)
            away = tcol - owner
            away = away + jnp.where(away < 0, float(dom_size), 0.0)
            near = away + HALF
            near = near - jnp.where(near >= dom_size, float(dom_size), 0.0)
            reach = jnp.where(away == far, float(HOOD - 1), near)
            reach = jnp.where(dcol >= 0, reach, -1.0)
            place = jnp.where(
                dcol >= 0, reach * (rep_size * slot_rows) + rank * cols, -1.0e6
            )
            tile = dcol - tiles * tcol
            spread = jnp.where(iota((panels, panels * rhs), 0) == lane_panel, place, 0.0)
            goal = jnp.sum(spread, axis=0, keepdims=True) + lane_row
            pack[l] = jnp.where(
                iota((senders * slot_rows, panels * rhs), 0) == goal, 1.0, 0.0
            ).astype(BF16)
            mine = (rank == id_slot) & (id_level == l)
            for j in range(HOOD):
                found = jnp.where(mine & (reach == j), tile + 1.0, 0.0)
                wanted[j] = wanted[j] + jnp.sum(found, axis=0, keepdims=True)
        for j in range(HOOD):
            row = jnp.where(wanted[j] > 0, (wanted[j] - 1.0) * cols + id_col, -1.0)
            id_send[j] = row.astype(jnp.int32)
        id_recv[HALF * rep_size + me_r] = id_send[HALF]

    def learn_ids():
        for j, step in peers:
            await_id(j, step)
        row_of = iota((senders, 128), 0)
        ids = jnp.zeros((senders, 128), F32)
        for s in range(senders):
            ids = jnp.where(row_of == s, id_recv[s].astype(F32), ids)
        ids = ids.astype(BF16)
        span = senders * slot_rows
        lane_sender = lanes_ref[2:3, :span]
        lane_in = lanes_ref[5:6, :span]
        for l in range(levels - 1):
            take = jnp.where(iota((128, span), 0) == lane_in + l * slot_rows, 1.0, 0.0)
            every = jnp.dot(ids, take.astype(BF16), preferred_element_type=F32)
            own = jnp.where(iota((senders, span), 0) == lane_sender, every, 0.0)
            goal = jnp.sum(own, axis=0, keepdims=True)
            unpack[l] = jnp.where(iota((tile_rows, span), 0) == goal, 1.0, 0.0).astype(BF16)

    def solve(level, residual):
        row_tile = lax.broadcasted_iota(jnp.int32, (tile_rows, width), 0)
        total = jnp.zeros((tile_rows, width), F32)
        for t in range(tiles):
            inside = (row_tile >= t * cols) & (row_tile < (t + 1) * cols)
            part = jnp.where(inside, residual, 0.0).astype(BF16)
            total = total + jnp.dot(part, diag[level, t], preferred_element_type=F32)
        return total

    route()
    pl.semaphore_wait(barrier, len(peers))

    for level in range(levels):
        residual = rs_ref[level]
        if level > 0:
            for j, step in peers:
                await_val(level - 1, j, step)
            arrived = val_recv[level - 1].reshape(senders * slot_rows, width)
            residual = residual - jnp.dot(
                unpack[level - 1], arrived, preferred_element_type=F32
            )
        load_diag(level).wait()
        solved = solve(level, residual)
        out_ref[level] = solved
        if level + 1 == levels:
            break
        rounded = solved.astype(BF16)
        solved_send[level, tile_span] = rounded
        for step in range(1, rep_size):
            send_solved(level, step).start()
        solved_recv[level, me_r, tile_span] = rounded
        if level == 0:
            for part in range(panels // chunk):
                load_panel(0, part).start()
            for j, step in peers:
                send_id(j, step).start()
        for step in range(1, rep_size):
            await_solved(level, step)
        gathered = jnp.dot(
            regroup_ref[...],
            solved_recv[level].reshape(rep_size * group_rows, width),
            preferred_element_type=F32,
        ).astype(BF16)
        store[level * tiles : (level + 1) * tiles] = gathered.reshape(tiles, rhs, width)
        for part in range(panels // chunk):
            load_panel(level, part).wait()
            for p in range(part * chunk, (part + 1) * chunk):
                source = store[src_ref[level, p]]
                product = jnp.dot(source, panel[level, p], preferred_element_type=F32)
                contrib[p * rhs : (p + 1) * rhs] = product.astype(BF16)
        packed = jnp.dot(pack[level], contrib[...], preferred_element_type=F32).astype(BF16)
        val_send[level] = packed.reshape(senders, slot_rows, width)
        for j, step in peers:
            send_val(level, j, step).start()
        own_slot = HALF * rep_size + me_r
        val_recv[level, own_slot] = val_send[level, own_slot]
        load_diag(level + 1).start()
        if level + 2 < levels:
            for part in range(panels // chunk):
                load_panel(level + 1, part).start()
        if level == 0:
            learn_ids()

    for j, step in peers:
        send_id(j, step).wait_send()
        for level in range(levels - 1):
            send_val(level, j, step).wait_send()
    for step in range(1, rep_size):
        for level in range(levels - 1):
            send_solved(level, step).wait_send()


def per_device(right_sides, diag_inverse, panel_mats, panel_src, panel_dst):
    levels, tiles, cols, width = right_sides.shape
    panels = panel_mats.shape[1]
    dom_size = lax.axis_size("dom")
    rep_size = lax.axis_size("rep")
    rhs = rep_size * cols
    tile_rows = tiles * cols
    slot_rows = round_up(SLOTS * cols, 16)
    group_rows = round_up(tile_rows, 16)
    senders = HOOD * rep_size
    chunk = 4 if panels % 4 == 0 else 1
    assert (levels - 1) * slot_rows <= 128
    dims = (
        levels, tiles, cols, width, panels, dom_size, rep_size, slot_rows, group_rows, chunk
    )
    lanes = jnp.asarray(lane_tables(rep_size, panels, cols, slot_rows))
    regroup = jnp.asarray(regroup_table(rep_size, tiles, cols, group_rows), BF16)
    vmem = pl.BlockSpec(memory_space=pltpu.VMEM)
    hbm = pl.BlockSpec(memory_space=pl.ANY)
    dma = pltpu.SemaphoreType.DMA
    solved = pl.pallas_call(
        functools.partial(kernel, dims),
        out_shape=jax.ShapeDtypeStruct((levels, tile_rows, width), F32),
        in_specs=[pl.BlockSpec(memory_space=pltpu.SMEM), vmem, vmem, vmem, vmem, hbm, hbm],
        out_specs=vmem,
        scratch_shapes=[
            pltpu.VMEM(diag_inverse.shape, BF16),
            pltpu.VMEM(panel_mats.shape, BF16),
            pltpu.VMEM(((levels - 1) * tiles, rhs, width), BF16),
            pltpu.VMEM((panels * rhs, width), BF16),
            pltpu.VMEM((levels - 1, senders * slot_rows, panels * rhs), BF16),
            pltpu.VMEM((levels - 1, tile_rows, senders * slot_rows), BF16),
            pltpu.VMEM((levels - 1, group_rows, width), BF16),
            pltpu.VMEM((levels - 1, rep_size, group_rows, width), BF16),
            pltpu.VMEM((levels - 1, senders, slot_rows, width), BF16),
            pltpu.VMEM((levels - 1, senders, slot_rows, width), BF16),
            pltpu.VMEM((HOOD, 1, 128), jnp.int32),
            pltpu.VMEM((senders, 1, 128), jnp.int32),
            dma((levels,)),
            dma((levels - 1, panels // chunk)),
            dma((levels - 1, rep_size)),
            dma((levels - 1, rep_size)),
            dma((levels - 1, senders)),
            dma((levels - 1, senders)),
            dma((senders,)),
            dma((senders,)),
        ],
        compiler_params=pltpu.CompilerParams(
            collective_id=0, has_side_effects=True, vmem_limit_bytes=56 * 1024 * 1024
        ),
    )(
        panel_src,
        panel_dst,
        right_sides.reshape(levels, tile_rows, width),
        lanes,
        regroup,
        diag_inverse,
        panel_mats,
    )
    return solved.reshape(right_sides.shape)


def solution(mesh):
    return jax.shard_map(
        per_device,
        mesh=mesh,
        in_specs=(
            P(None, "dom", "rep", None),
            P(None, "dom", None, None),
            P(None, ("dom", "rep"), None, None),
            P(None, ("dom", "rep")),
            P(None, ("dom", "rep")),
        ),
        out_specs=P(None, "dom", "rep", None),
        check_vma=False,
    )
```

time: 157 us -> 54.3 us (0.35)
  starting transfers between devices: 64.1 us -> 0 us
  Pallas kernels: 0 us -> 50.9 us
  blocking collectives: 41.1 us -> 0 us
  matrix products: 22.9 us -> 0 us
  waiting for transfers between devices: 12.3 us -> 0 us
  local copies, waits for them, and re-layouts: 9.84 us -> 3.23 us
  other arithmetic: 5.2 us -> 0 us
    pallas_call x0 -> x1, Pallas kernels: none -> 50.9 us  [per_device(): pl.pallas_call(functools.partial(kernel, dims), out_shape=jax.ShapeDtypeS...]
    all_gather x3 -> x0, blocking collectives: 41.1 us -> none  [per_device(): lax.all_gather(solved.astype(jnp.bfloat16), 'rep', axis=1, tiled=True)]
    ppermute x30 -> x0, starting transfers between devices: 33.9 us -> none  [passed_along(): lax.ppermute(value, axis, [(i, (i + by) % size) for i in range(size)])]
    all_to_all x6 -> x0, starting transfers between devices: 30.2 us -> none  [the longest x3 16.5 us: deliver(): lax.all_to_all(slot_ids.astype(jnp.bfloat16), 'rep', split_axis=2, concat...]
    dot_general x28 -> x0, matrix products: 22.9 us -> none  [the longest x3 9.38 us: panel_updates(): jnp.einsum('pcx,pxy->pcy', sources, matrices, preferred_element_type=jnp....]
    ppermute x30 -> x0, waiting for transfers between devices: 12.3 us -> none  [passed_along(): lax.ppermute(value, axis, [(i, (i + by) % size) for i in range(size)])]
    reshape x3 -> x2, local copies, waits for them, and re-layouts: 0.41 us -> 3.23 us  [the longest x1 1.62 us: per_device(): right_sides.reshape(levels, tile_rows, width)]
    convert_element_type x24 -> x0, local copies, waits for them, and re-layouts: 2.79 us -> none  [the longest x3 2.3 us: deliver(): slot_vals.astype(jnp.bfloat16)]
  transfers between devices with their start and end apart: 36 -> 0, of which waited for: 13 -> 0; matrix products, arithmetic and copies ran while one was open for 19% -> 0% of each run, Pallas kernels for 0% -> 0%
where the time goes in v1:
time: 54.3 us; the launch traced here: 54.1 us
  Pallas kernels  50.9 us (94%)
  local copies, waits for them, and re-layouts  3.23 us (6%)
    pallas_call x1, Pallas kernels, per_device(): pl.pallas_call(functools.partial(kernel, dims), out_shape=jax.ShapeDtypeS...  50.9 us
    reshape x1, local copies, waits for them, and re-layouts, per_device(): right_sides.reshape(levels, tile_rows, width)  1.62 us
    reshape x1, local copies, waits for them, and re-layouts, per_device(): return solved.reshape(right_sides.shape)  1.61 us

profile of v1, /device:TPU:0, one launch (start us, length us, event | category | flops | bytes accessed | tf_op | source)
XLA Modules:
  0.0 54.1 jit_solution(11654009014409407250)
XLA Ops:
  0.0 1.6 %reshape.6.rs_ref = f32[4,24,384]{2,1,0:T(8,128)} reshape(f32[4,6,4,384]{3,2,1,0:T(4,128)} %param.7) | data formatting | bytes 294912 | tf_op jit(solution)/shard_map/reshape | solution.py:356
  1.6 50.9 %shard_map.73 = f32[4,24,384]{2,1,0:T(8,128)} custom-call(s32[3,16]{1,0:T(4,128)} %src_ref.1, s32[3,16]{1,0:T(4,128)} %dst_ref.1, f32[4,24,384]{2,1,0:T(8,128)} %reshape.6.rs_ref, f32[8,384]{1,0:T(8,128)} %constant.4.clone.lanes_ref, bf16[96,128]{1,0:T(8,128)(2,1)} %constant.5.clone.regroup_ref, bf16[4,6,384,384]{3,2,1,0:T(8,128)(2,1)} %diag_hbm.1, ...), custom_call_target="tpu_custom_call" | custom-call | tf_op jit(solution)/shard_map/pallas_call | solution.py:323
  52.5 1.6 %reshape.7 = f32[4,6,4,384]{3,2,1,0:T(4,128)} reshape(f32[4,24,384]{2,1,0:T(8,128)} %shard_map.73) | data formatting | bytes 294912 | tf_op jit(solution)/shard_map/reshape | solution.py:362
